TPU v7x, 32 devices: a whole 2x2x4 slice. The times are simulated.
32 devices in a mesh: dp: 4 (over z), ctx: 4 (over y, core), tp: 2 (over x).
Axes of the slice: x: 2, y: 2, z: 4, core: 2. Of those that a mesh axis runs over, the one named last changes fastest.
Arguments:
- queries: bfloat16 [4, 512, 4096], P('dp', 'ctx', 'tp'), may hold values from -8 to 8
- keys_text: bfloat16 [4, 512, 512], P('dp', 'ctx', 'tp'), may hold values from -8 to 8
- values_text: bfloat16 [4, 512, 512], P('dp', 'ctx', 'tp'), may hold values from -6 to 6
- patch_rows: bfloat16 [4, 4, 8, 2, 512], P('dp', 'ctx', None, None, 'tp'), may hold values from -6 to 6
- patch_owner: int32 [4, 4, 8, 1], P('dp', 'ctx'), may hold values from 0 to 3; in each aligned block of 8 rows (0 to 7, 8 to 15, ..., all dimensions but the last counted through in order) at most 4 rows name the same one
- patch_place: int32 [4, 4, 8], P('dp', 'ctx'), may hold values from 0 to 127
- value_head: bfloat16 [4096], P('tp'), may hold values from -0.75 to 0.75
Outputs:
- attention: bfloat16 [4, 512, 4096], P('dp', 'ctx', 'tp')
- value_out: float32 [4, 512], P('dp', 'ctx')
Inputs may be any that keep to these rules, and one draw needn't show every extreme that they name: `patch_owner`: among the rows of one vision shard at most 4 name the same sequence, and exactly 4 do in some shards. `patch_place`: rows that share an owner, a ctx index and a position are all added there.
All inputs are finite; a program needn't handle non-finite values.
Results may differ from a plain program's by a relative error of at most 0.0079.
Values may be sent and summed in bfloat16 or wider, within the bound.
A program may use at most 64 MiB of HBM per device.

v0:
```python
import jax
import jax.numpy as jnp
from jax import lax
from jax.sharding import PartitionSpec as P

HD = 128
CAP = 4


def attend_block(
    carried, query_split, query_place, block_keys, block_values, key_place, score_scale
):
    running_max, denominator, numerator = carried
    scores = (
        jnp.einsum("tgrd,sgd->tgrs", query_split, block_keys, preferred_element_type=jnp.float32)
        * score_scale
    )
    allowed = (key_place[None, :] <= query_place[:, None])[:, None, None, :]
    scores = jnp.where(allowed, scores, -1e30)
    new_max = jnp.maximum(running_max, jnp.max(scores, axis=-1))
    weights = jnp.where(allowed, jnp.exp(scores - new_max[..., None]), 0.0)
    shrink = jnp.exp(running_max - new_max)
    denominator = denominator * shrink + jnp.sum(weights, axis=-1)
    numerator = numerator * shrink[..., None] + jnp.einsum(
        "tgrs,sgd->tgrd",
        weights.astype(jnp.bfloat16),
        block_values,
        preferred_element_type=jnp.float32,
    )
    return (new_max, denominator, numerator)


def unchanged(carried):
    return carried


def body(queries, keys_text, values_text, patch_rows, patch_owner, patch_place, value_head):
    token_count = queries.shape[1]
    kv_width = keys_text.shape[2]
    groups = kv_width // HD
    head_count = queries.shape[2] // HD
    group_size = head_count // groups
    score_scale = HD ** (-0.5)
    dp_count = lax.axis_size("dp")
    slot_count = dp_count * CAP
    owner_seq = patch_owner[0, 0, :, 0]
    places = patch_place[0, 0]
    owner_hits = (owner_seq[:, None] == jnp.arange(dp_count, dtype=jnp.int32)[None, :]).astype(
        jnp.int32
    )
    before = jnp.cumsum(owner_hits, axis=0) - owner_hits
    slot_rank = jnp.sum(before * owner_hits, axis=1)
    target = owner_seq * CAP + slot_rank
    select = (jnp.arange(slot_count, dtype=jnp.int32)[:, None] == target[None, :]).astype(jnp.int32)
    row_data = patch_rows[0, 0].reshape(places.shape[0], 2 * kv_width)
    packed = jnp.dot(
        select.astype(jnp.bfloat16), row_data, preferred_element_type=jnp.float32
    ).astype(jnp.bfloat16)
    filled = jnp.sum(select, axis=1)
    slot_place = jnp.sum(select * places[None, :], axis=1) + (1 - filled) * token_count
    packed = packed.reshape(slot_count, 2, kv_width)
    arrived, arrived_place = (
        lax.all_to_all(packed, "dp", split_axis=0, concat_axis=0, tiled=True),
        lax.all_to_all(slot_place, "dp", split_axis=0, concat_axis=0, tiled=True),
    )
    landing = (jnp.arange(token_count, dtype=jnp.int32)[:, None] == arrived_place[None, :]).astype(
        jnp.bfloat16
    )
    arrivals = jnp.dot(
        landing, arrived.reshape(slot_count, 2 * kv_width), preferred_element_type=jnp.float32
    )
    merged_keys = (keys_text[0].astype(jnp.float32) + arrivals[:, :kv_width]).astype(jnp.bfloat16)
    merged_values = (values_text[0].astype(jnp.float32) + arrivals[:, kv_width:]).astype(
        jnp.bfloat16
    )
    query_split = queries[0].reshape(token_count, groups, group_size, HD)
    first_row = lax.axis_index("ctx") * token_count
    query_place = first_row + jnp.arange(token_count, dtype=jnp.int32)
    initial = (
        jnp.full((token_count, groups, group_size), -1e30, jnp.float32),
        jnp.zeros((token_count, groups, group_size), jnp.float32),
        jnp.zeros((token_count, groups, group_size, HD), jnp.float32),
    )
    carried = initial
    start_row = jnp.int32(0)
    piece_keys = lax.all_gather(merged_keys, "ctx", axis=0, tiled=True)
    piece_values = lax.all_gather(merged_values, "ctx", axis=0, tiled=True)
    piece_rows = piece_keys.shape[0]
    block_rows = min(512, piece_rows)
    for lower in range(0, piece_rows, block_rows):
        upper = min(lower + block_rows, piece_rows)
        block_keys = piece_keys[lower:upper].reshape(upper - lower, groups, HD)
        block_values = piece_values[lower:upper].reshape(upper - lower, groups, HD)
        key_place = start_row + lower + jnp.arange(upper - lower, dtype=jnp.int32)

        def update(state_in):
            return attend_block(
                state_in, query_split, query_place, block_keys, block_values, key_place, score_scale
            )

        carried = lax.cond(
            start_row + lower <= first_row + token_count - 1, update, unchanged, carried
        )
    running_max, denominator, numerator = carried
    attention = (
        (numerator / denominator[..., None])
        .reshape(token_count, head_count * HD)
        .astype(jnp.bfloat16)
    )
    partial_value = jnp.dot(attention, value_head, preferred_element_type=jnp.float32)
    value_out = lax.psum(partial_value, "tp")
    return (attention[None], value_out[None])


def solution(mesh):
    in_specs = (
        P("dp", "ctx", "tp"),
        P("dp", "ctx", "tp"),
        P("dp", "ctx", "tp"),
        P("dp", "ctx", None, None, "tp"),
        P("dp", "ctx", None, None),
        P("dp", "ctx", None),
        P("tp"),
    )
    out_specs = (P("dp", "ctx", "tp"), P("dp", "ctx"))
    return jax.shard_map(body, mesh=mesh, in_specs=in_specs, out_specs=out_specs, check_vma=False)
```

profile of v0, /device:TPU:0, one launch (start us, length us, event | category | flops | bytes accessed | tf_op | source)
XLA Modules:
  0.0 53.5 jit_solution(15466480431015100622)
XLA Ops:
  0.6 0.7 %fusion.25 = s32[8,4]{0,1:T(4,128)S(1)} fusion(s32[8]{0:T(128)} %bitcast.58), kind=kLoop, calls=%fused_computation.37 | loop fusion | flops 64 | bytes 160 | tf_op jit(solution)/shard_map/convert_element_type | solution.py:48
  1.3 0.2 reduce_window_sum.11
  1.5 0.7 %select_reduce_fusion.1 = s32[8]{0:T(128)S(1)} fusion(s32[8,4]{0,1:T(4,128)S(1)} %reduce_window_sum.11, s32[8]{0:T(128)} %bitcast.59), kind=kLoop, calls=%fused_computation.35 | loop fusion | flops 152 | bytes 192 | tf_op jit(solution)/shard_map/reduce_sum | solution.py:52
  2.2 0.7 %multiply_add_fusion.1 = s32[8]{0:T(128)S(1)} fusion(s32[8]{0:T(128)S(1)} %select_reduce_fusion.1, s32[1,1,8,1]{2,3,1,0:T(1,128)} %param.13), kind=kLoop, calls=%fused_computation.39 | loop fusion | flops 16 | bytes 96 | tf_op jit(solution)/shard_map/add | solution.py:53
  2.8 0.7 %convert_reduce_fusion = (s32[16]{0:T(128)S(1)}, s32[16]{0:T(128)S(1)}) fusion(s32[8]{0:T(128)S(1)} %multiply_add_fusion.1, s32[8]{0:T(128)} %bitcast.60), kind=kLoop, calls=%fused_computation.31 | loop fusion | flops 608 | bytes 192 | tf_op jit(solution)/shard_map/reduce_sum | solution.py:59
  3.6 0.7 %add.48 = s32[4,4,1]{1,0,2:T(4,128)} reshape(s32[16]{0:T(128)S(1)} %multiply_add_fusion) | data formatting | bytes 128 | tf_op jit(solution)/shard_map/add | solution.py:60
  4.2 6.3 %all-to-all-start = ((s32[4,4,1]{1,2,0:T(1,128)}), s32[4,4,1]{1,2,0:T(1,128)S(1)}, u32[]{:S(2)}, u32[]{:S(2)}) async-start(s32[4,4,1]{1,2,0:T(1,128)} %bitcast.7), calls=%async_computation | async-start | bytes 4096 | tf_op jit(solution)/shard_map/all_to_all | solution.py:64
  10.6 0.7 %copy.45 = bf16[1,8,2,256]{3,1,2,0:T(8,128)(2,1)S(1)} copy(bf16[1,8,2,256]{3,2,1,0:T(2,128)(2,1)} %bitcast.56) | data formatting | bytes 16384
  11.3 0.3 convolution_convert_fusion
  11.5 0.6 %reshape.108 = bf16[16,2,256]{2,1,0:T(2,128)(2,1)} reshape(bf16[16,512]{1,0:T(8,128)(2,1)S(1)} %convolution_convert_fusion) | data formatting | bytes 32768 | tf_op jit(solution)/shard_map/reshape | solution.py:61
  12.2 3.8 %all-to-all-done = s32[4,4,1]{1,2,0:T(1,128)S(1)} async-done(((s32[4,4,1]{1,2,0:T(1,128)}), s32[4,4,1]{1,2,0:T(1,128)S(1)}, u32[]{:S(2)}, u32[]{:S(2)}) %all-to-all-start) | async-done | bytes 96 | tf_op jit(solution)/shard_map/all_to_all | solution.py:64
  16.0 3.3 %all-to-all-start.1 = ((bf16[16,2,256]{2,1,0:T(2,128)(2,1)}), bf16[16,2,256]{2,1,0:T(2,128)(2,1)S(1)}, u32[]{:S(2)}, u32[]{:S(2)}) async-start(bf16[16,2,256]{2,1,0:T(2,128)(2,1)} %reshape.108), calls=%async_computation.1 | async-start | bytes 32768 | tf_op jit(solution)/shard_map/all_to_all | solution.py:63
  19.3 0.7 %reshape.114 = bf16[2048,1]{0,1:T(2,128)(2,1)S(1)} reshape(bf16[2048]{0:T(1024)(128)(2,1)} %param.15) | data formatting | bytes 8192 | tf_op args[6]
  20.0 0.6 %broadcast.91 = s32[]{:T(128)} broadcast(s32[]{:T(128)} %constant.11.clone.1), dimensions={} | broadcast | bytes 8 | tf_op jit(solution)/shard_map/all_to_all | solution.py:64
  20.6 0.7 %reduce.3 = s32[4,4]{1,0:T(4,128)S(1)} reduce(s32[4,4,1]{1,2,0:T(1,128)S(1)} %all-to-all-done, s32[]{:T(128)} %broadcast.91), dimensions={2}, to_apply=%all_to_all.7.reduce_sub_computation.3 | reduce | bytes 132 | tf_op jit(solution)/shard_map/all_to_all | solution.py:64
  21.3 0.1 eq.48
  21.4 3.5 %all-to-all-done.1 = bf16[16,2,256]{2,1,0:T(2,128)(2,1)S(1)} async-done(((bf16[16,2,256]{2,1,0:T(2,128)(2,1)}), bf16[16,2,256]{2,1,0:T(2,128)(2,1)S(1)}, u32[]{:S(2)}, u32[]{:S(2)}) %all-to-all-start.1) | async-done | bytes 16416 | tf_op jit(solution)/shard_map/all_to_all | solution.py:63
  24.9 0.2 fusion.22
  25.0 0.9 %fusion.20 = (bf16[128,256]{1,0:T(8,128)(2,1)S(1)}, bf16[128,256]{1,0:T(8,128)(2,1)S(1)}) fusion(f32[128,512]{1,0:T(8,128)S(1)} %fusion.22, bf16[1,128,256]{2,1,0:T(8,128)(2,1)} %param.11, bf16[1,128,256]{2,1,0:T(8,128)(2,1)} %param.10), kind=kLoop, calls=%fused_computation.24 | loop fusion | flops 196608 | bytes 524288 | tf_op jit(solution)/shard_map/convert_element_type | solution.py:73
  25.9 5.8 %all_gather.6 = bf16[512,256]{1,0:T(8,128)(2,1)S(1)} all-gather(bf16[128,256]{1,0:T(8,128)(2,1)S(1)} %get-tuple-element.45), channel_id=1, replica_groups=mesh['dp'=4,'ctx'=4,'tp'=2] {'ctx'}, dimensions={0}, use_global_device_ids=true | all-gather | bytes 327680 | tf_op jit(solution)/shard_map/all_gather | solution.py:86
  31.7 5.8 %all_gather.7 = bf16[512,256]{1,0:T(8,128)(2,1)S(1)} all-gather(bf16[128,256]{1,0:T(8,128)(2,1)S(1)} %get-tuple-element.44), channel_id=1, replica_groups=mesh['dp'=4,'ctx'=4,'tp'=2] {'ctx'}, dimensions={0}, use_global_device_ids=true | all-gather | bytes 327680 | tf_op jit(solution)/shard_map/all_gather | solution.py:87
  37.6 9.2 %conditional.1 = (f32[128,2,8]{0,2,1:T(8,128)S(1)}, f32[128,2,8,128]{0,3,2,1:T(8,128)S(1)}) conditional(s32[]{:T(128)} %convert_element_type.53, () %tuple.16, (s32[512]{0:T(512)S(1)}, s32[]{:T(128)}, s32[128]{0:T(128)S(1)}, bf16[512,256]{1,0:T(8,128)(2,1)S(1)}, bf16[1,128,2048]{2,1,0:T(8,128)(2,1)}, /*index=5*/bf16[512,256]{1,0:T(8,128)(2,1)S(1)}) %tuple.17), branch_computations={%region_4.5_spmd, %region_5.8_spmd} | conditional | flops 550836352 | bytes 36007472 | solution.py:101
  37.6 0.1 broadcast_compare_fusion
  37.7 1.1 %copy.44 = bf16[16,8,16,128]{3,2,1,0:T(8,128)(2,1)S(1)} copy(bf16[16,8,16,128]{3,1,2,0:T(8,128)(2,1)} %bitcast.52) | data formatting | bytes 1048576 | tf_op jit(solution)/shard_map/cond
  38.9 0.1 reshape.104
  38.9 0.8 %fusion = (f32[128,2,8]{0,2,1:T(8,128)S(1)}, f32[2,512,128,8]{2,1,3,0:T(8,128)S(1)}) fusion(pred[128,512]{0,1:T(8,128)(4,1)S(1)} %broadcast_compare_fusion, bf16[128,2,8,128]{3,2,1,0:T(8,128)(2,1)S(1)} %bitcast.50, bf16[512,2,128,1]{2,1,0,3:T(2,128)(2,1)S(1)} %bitcast.51), kind=kOutput, calls=%fused_computation.2 | convolution fusion | flops 271579136 | bytes 5054464 | tf_op jit(solution)/shard_map/cond/branch_1_fun/tgrd,sgd->tgrs/dot_general | solution.py:15
  39.7 0.0 copy-start
  39.7 1.9 %copy-done = f32[2,512,128,8]{2,1,3,0:T(8,128)} copy-done((f32[2,512,128,8]{2,1,3,0:T(8,128)}, f32[2,512,128,8]{2,1,3,0:T(8,128)S(1)}, u32[]{:S(2)}) %copy-start) | copy-done | bytes 4194328 | tf_op jit(solution)/shard_map/cond
  41.7 1.0 %fusion.2 = f32[128,2,8]{0,2,1:T(8,128)S(1)} fusion(f32[2,512,128,8]{2,1,3,0:T(8,128)S(1)} %get-tuple-element.43, f32[128,2,8]{0,2,1:T(8,128)S(1)} %broadcast_maximum_fusion, pred[128,512]{0,1:T(8,128)(4,1)S(1)} %broadcast_compare_fusion), kind=kLoop, calls=%fused_computation.4 | loop fusion | flops 5240832 | bytes 4276224 | tf_op jit(solution)/shard_map/cond/branch_1_fun/reduce_sum | solution.py:23
  42.7 0.1 reshape.105
  42.8 3.7 %fusion.9 = f32[128,2,8,128]{3,0,2,1:T(8,128)S(1)} fusion(f32[2,512,128,8]{2,1,3,0:T(8,128)} %copy-done, f32[128,2,8]{0,2,1:T(8,128)S(1)} %broadcast_maximum_fusion, pred[128,512]{0,1:T(8,128)(4,1)S(1)} %broadcast_compare_fusion, f32[128,2,8]{0,2,1:T(8,128)S(1)} %get-tuple-element.40, bf16[512,2,128,1]{2,1,0,3:T(2,128)(2,1)S(1)} %bitcast.53), kind=kOutput, calls=%fused_computation.8 | convolution fusion | flops 273940480 | bytes 5586944 | tf_op jit(solution)/shard_map/cond/branch_1_fun/tgrs,sgd->tgrd/dot_general | solution.py:24
  46.5 0.3 copy.43
  46.8 0.1 divide_convert_fusion
  46.9 1.0 %copy.34 = bf16[1,128,2048]{2,1,0:T(8,128)(2,1)} copy(bf16[1,128,2048]{1,2,0:T(8,128)(2,1)S(1)} %bitcast.48) | data formatting | bytes 1048576
  47.9 0.2 fusion.26
  48.1 5.4 %psum.7 = f32[1,128]{1,0:T(1,128)} all-reduce(f32[1,128]{1,0:T(1,128)S(1)} %fusion.26), channel_id=1, replica_groups=mesh['dp'=4,'ctx'=4,'tp'=2] {'tp'}, use_global_device_ids=true, to_apply=%region_8.9 | all-reduce | flops 128 | bytes 1024 | tf_op jit(solution)/shard_map/psum | solution.py:111
  (7 shorter events, 0.0 us)
Async XLA Ops:
  4.2 11.8 %all-to-all-start = ((s32[4,4,1]{1,2,0:T(1,128)}), s32[4,4,1]{1,2,0:T(1,128)S(1)}, u32[]{:S(2)}, u32[]{:S(2)}) async-start(s32[4,4,1]{1,2,0:T(1,128)} %bitcast.7), calls=%async_computation | async-start | bytes 4096 | tf_op jit(solution)/shard_map/all_to_all | solution.py:64
  16.0 8.8 %all-to-all-start.1 = ((bf16[16,2,256]{2,1,0:T(2,128)(2,1)}), bf16[16,2,256]{2,1,0:T(2,128)(2,1)S(1)}, u32[]{:S(2)}, u32[]{:S(2)}) async-start(bf16[16,2,256]{2,1,0:T(2,128)(2,1)} %reshape.108), calls=%async_computation.1 | async-start | bytes 32768 | tf_op jit(solution)/shard_map/all_to_all | solution.py:63
  39.7 1.9 %copy-start = (f32[2,512,128,8]{2,1,3,0:T(8,128)}, f32[2,512,128,8]{2,1,3,0:T(8,128)S(1)}, u32[]{:S(2)}) copy-start(f32[2,512,128,8]{2,1,3,0:T(8,128)S(1)} %get-tuple-element.43) | copy-start | bytes 12582916 | tf_op jit(solution)/shard_map/cond
where the time goes:
time: 54.1 us; the launch traced here: 53.5 us
  blocking collectives  17 us (31%)
  starting transfers between devices  9.6 us (18%)
  local copies, waits for them, and re-layouts  7.91 us (15%)
  waiting for transfers between devices  7.34 us (14%)
  other arithmetic  5.85 us (11%)
  matrix products  5.05 us (9%)
  between operations  0.68 us (1%)
    all_to_all x1, starting transfers between devices, body(): lax.all_to_all(slot_place, 'dp', split_axis=0, concat_axis=0, tiled=True)  6.35 us
    all_gather x1, blocking collectives, body(): piece_values = lax.all_gather(merged_values, 'ctx', axis=0, tiled=True)  5.84 us
    all_gather x1, blocking collectives, body(): piece_keys = lax.all_gather(merged_keys, 'ctx', axis=0, tiled=True)  5.78 us
    psum x1, blocking collectives, body(): value_out = lax.psum(partial_value, 'tp')  5.42 us
    all_to_all x1, waiting for transfers between devices, body(): lax.all_to_all(slot_place, 'dp', split_axis=0, concat_axis=0, tiled=True)  3.85 us
    dot_general x1, matrix products, attend_block(): jnp.einsum('tgrs,sgd->tgrd', weights.astype(jnp.bfloat16), block_values,...  3.67 us
    all_to_all x1, waiting for transfers between devices, body(): lax.all_to_all(packed, 'dp', split_axis=0, concat_axis=0, tiled=True)  3.49 us
    all_to_all x1, starting transfers between devices, body(): lax.all_to_all(packed, 'dp', split_axis=0, concat_axis=0, tiled=True)  3.25 us
  transfers between devices with their start and end apart: 2, of which 2 were waited for; matrix products, arithmetic and copies ran while one was open for 7% of the time, Pallas kernels for 0%

commit v1 on v0

--- a/solution.py
+++ b/solution.py
@@ -83,8 +83,9 @@
     )
     carried = initial
     start_row = jnp.int32(0)
-    piece_keys = lax.all_gather(merged_keys, "ctx", axis=0, tiled=True)
-    piece_values = lax.all_gather(merged_values, "ctx", axis=0, tiled=True)
+    spare = jnp.concatenate([merged_keys, merged_values], 1)
+    outcome_arr = lax.all_gather(spare, "ctx", axis=0, tiled=True)
+    piece_keys, piece_values = jnp.split(outcome_arr, [merged_keys.shape[1]], 1)
     piece_rows = piece_keys.shape[0]
     block_rows = min(512, piece_rows)
     for lower in range(0, piece_rows, block_rows):

time: 54.1 us -> 45.7 us (0.84)
  blocking collectives: 17 us -> 12.6 us
  matrix products: 5.05 us -> 2.94 us
  local copies, waits for them, and re-layouts: 7.91 us -> 6.03 us
    all_gather x2 -> x1, blocking collectives: 11.6 us -> 7.2 us  [body(): outcome_arr = lax.all_gather(spare, 'ctx', axis=0, tiled=True)]
    dot_general x1, matrix products: 3.67 us -> 1.47 us  [attend_block(): jnp.einsum('tgrs,sgd->tgrd', weights.astype(jnp.bfloat16), block_values,...]
    cond x3 -> x1, local copies, waits for them, and re-layouts: 3.05 us -> 1.15 us
  transfers between devices with their start and end apart: 2 -> 2, of which waited for: 2 -> 2; matrix products, arithmetic and copies ran while one was open for 7% -> 8% of each run, Pallas kernels for 0% -> 0%
where the time goes in v1:
time: 45.7 us; the launch traced here: 45.2 us
  blocking collectives  12.6 us (28%)
  starting transfers between devices  9.6 us (21%)
  waiting for transfers between devices  7.56 us (17%)
  local copies, waits for them, and re-layouts  6.03 us (13%)
  other arithmetic  5.7 us (12%)
  matrix products  2.94 us (6%)
  between operations  0.69 us (2%)
    all_gather x1, blocking collectives, body(): outcome_arr = lax.all_gather(spare, 'ctx', axis=0, tiled=True)  7.2 us
    all_to_all x1, starting transfers between devices, body(): lax.all_to_all(slot_place, 'dp', split_axis=0, concat_axis=0, tiled=True)  6.35 us
    psum x1, blocking collectives, body(): value_out = lax.psum(partial_value, 'tp')  5.42 us
    all_to_all x1, waiting for transfers between devices, body(): lax.all_to_all(slot_place, 'dp', split_axis=0, concat_axis=0, tiled=True)  3.85 us
    all_to_all x1, waiting for transfers between devices, body(): lax.all_to_all(packed, 'dp', split_axis=0, concat_axis=0, tiled=True)  3.71 us
    all_to_all x1, starting transfers between devices, body(): lax.all_to_all(packed, 'dp', split_axis=0, concat_axis=0, tiled=True)  3.25 us
    unnamed x4, local copies, waits for them, and re-layouts  2.41 us
    dot_general x1, matrix products, attend_block(): jnp.einsum('tgrs,sgd->tgrd', weights.astype(jnp.bfloat16), block_values,...  1.47 us
  transfers between devices with their start and end apart: 2, of which 2 were waited for; matrix products, arithmetic and copies ran while one was open for 8% of the time, Pallas kernels for 0%

profile of v1, /device:TPU:0, one launch (start us, length us, event | category | flops | bytes accessed | tf_op | source)
XLA Modules:
  0.0 45.2 jit_solution(2996413573991728077)
XLA Ops:
  0.6 0.7 %fusion.23 = s32[8,4]{0,1:T(4,128)S(1)} fusion(s32[8]{0:T(128)} %bitcast.68), kind=kLoop, calls=%fused_computation.36 | loop fusion | flops 64 | bytes 160 | tf_op jit(solution)/shard_map/convert_element_type | solution.py:48
  1.3 0.2 reduce_window_sum.11
  1.5 0.7 %select_reduce_fusion.1 = s32[8]{0:T(128)S(1)} fusion(s32[8,4]{0,1:T(4,128)S(1)} %reduce_window_sum.11, s32[8]{0:T(128)} %bitcast.69), kind=kLoop, calls=%fused_computation.34 | loop fusion | flops 152 | bytes 192 | tf_op jit(solution)/shard_map/reduce_sum | solution.py:52
  2.2 0.7 %multiply_add_fusion.1 = s32[8]{0:T(128)S(1)} fusion(s32[8]{0:T(128)S(1)} %select_reduce_fusion.1, s32[1,1,8,1]{2,3,1,0:T(1,128)} %param.13), kind=kLoop, calls=%fused_computation.38 | loop fusion | flops 16 | bytes 96 | tf_op jit(solution)/shard_map/add | solution.py:53
  2.8 0.7 %convert_reduce_fusion = (s32[16]{0:T(128)S(1)}, s32[16]{0:T(128)S(1)}) fusion(s32[8]{0:T(128)S(1)} %multiply_add_fusion.1, s32[8]{0:T(128)} %bitcast.70), kind=kLoop, calls=%fused_computation.30 | loop fusion | flops 608 | bytes 192 | tf_op jit(solution)/shard_map/reduce_sum | solution.py:59
  3.6 0.7 %add.48 = s32[4,4,1]{1,0,2:T(4,128)} reshape(s32[16]{0:T(128)S(1)} %multiply_add_fusion) | data formatting | bytes 128 | tf_op jit(solution)/shard_map/add | solution.py:60
  4.2 6.3 %all-to-all-start = ((s32[4,4,1]{1,2,0:T(1,128)}), s32[4,4,1]{1,2,0:T(1,128)S(1)}, u32[]{:S(2)}, u32[]{:S(2)}) async-start(s32[4,4,1]{1,2,0:T(1,128)} %bitcast.9), calls=%async_computation | async-start | bytes 4096 | tf_op jit(solution)/shard_map/all_to_all | solution.py:64
  10.6 0.7 %copy.46 = bf16[1,8,2,256]{3,1,2,0:T(8,128)(2,1)S(1)} copy(bf16[1,8,2,256]{3,2,1,0:T(2,128)(2,1)} %bitcast.66) | data formatting | bytes 16384
  11.3 0.3 convolution_convert_fusion
  11.5 0.6 %reshape.108 = bf16[16,2,256]{2,1,0:T(2,128)(2,1)} reshape(bf16[16,512]{1,0:T(8,128)(2,1)S(1)} %convolution_convert_fusion) | data formatting | bytes 32768 | tf_op jit(solution)/shard_map/reshape | solution.py:61
  12.2 3.8 %all-to-all-done = s32[4,4,1]{1,2,0:T(1,128)S(1)} async-done(((s32[4,4,1]{1,2,0:T(1,128)}), s32[4,4,1]{1,2,0:T(1,128)S(1)}, u32[]{:S(2)}, u32[]{:S(2)}) %all-to-all-start) | async-done | bytes 96 | tf_op jit(solution)/shard_map/all_to_all | solution.py:64
  16.0 3.3 %all-to-all-start.1 = ((bf16[16,2,256]{2,1,0:T(2,128)(2,1)}), bf16[16,2,256]{2,1,0:T(2,128)(2,1)S(1)}, u32[]{:S(2)}, u32[]{:S(2)}) async-start(bf16[16,2,256]{2,1,0:T(2,128)(2,1)} %reshape.108), calls=%async_computation.1 | async-start | bytes 32768 | tf_op jit(solution)/shard_map/all_to_all | solution.py:63
  19.3 0.7 %reshape.114 = bf16[2048,1]{0,1:T(2,128)(2,1)S(1)} reshape(bf16[2048]{0:T(1024)(128)(2,1)} %param.15) | data formatting | bytes 8192 | tf_op args[6]
  20.0 0.5 %broadcast.91 = s32[]{:T(128)} broadcast(s32[]{:T(128)} %constant.11.clone.1), dimensions={} | broadcast | bytes 8 | tf_op jit(solution)/shard_map/all_to_all | solution.py:64
  20.5 0.6 %reduce.3 = s32[4,4]{1,0:T(4,128)S(1)} reduce(s32[4,4,1]{1,2,0:T(1,128)S(1)} %all-to-all-done, s32[]{:T(128)} %broadcast.91), dimensions={2}, to_apply=%all_to_all.7.reduce_sub_computation.3 | reduce | bytes 132 | tf_op jit(solution)/shard_map/all_to_all | solution.py:64
  21.1 0.1 eq.48
  21.1 3.7 %all-to-all-done.1 = bf16[16,2,256]{2,1,0:T(2,128)(2,1)S(1)} async-done(((bf16[16,2,256]{2,1,0:T(2,128)(2,1)}), bf16[16,2,256]{2,1,0:T(2,128)(2,1)S(1)}, u32[]{:S(2)}, u32[]{:S(2)}) %all-to-all-start.1) | async-done | bytes 16416 | tf_op jit(solution)/shard_map/all_to_all | solution.py:63
  24.9 0.2 fusion.20
  25.0 0.9 %fusion.19 = (bf16[128,256]{1,0:T(8,128)(2,1)S(1)}, bf16[128,256]{1,0:T(8,128)(2,1)S(1)}) fusion(f32[128,512]{1,0:T(8,128)S(1)} %fusion.20, bf16[1,128,256]{2,1,0:T(8,128)(2,1)} %param.10, bf16[1,128,256]{2,1,0:T(8,128)(2,1)} %param.11), kind=kLoop, calls=%fused_computation.24 | loop fusion | flops 196608 | bytes 524288 | tf_op jit(solution)/shard_map/convert_element_type | solution.py:72
  25.9 7.2 %all_gather.3 = bf16[512,512]{1,0:T(8,128)(2,1)S(1)} all-gather(bf16[128,512]{1,0:T(8,128)(2,1)S(1)} %pad_maximum_fusion), channel_id=1, replica_groups=mesh['dp'=4,'ctx'=4,'tp'=2] {'ctx'}, dimensions={0}, use_global_device_ids=true | all-gather | bytes 655360 | tf_op jit(solution)/shard_map/all_gather | solution.py:87
  33.2 5.3 %conditional.1 = (f32[128,2,8]{0,2,1:T(8,128)S(1)}, f32[128,2,8,128]{0,3,2,1:T(8,128)S(1)}) conditional(s32[]{:T(128)} %convert_element_type.53, () %tuple.16, (s32[512]{0:T(512)S(1)}, s32[]{:T(128)}, s32[128]{0:T(128)S(1)}, bf16[512,512]{1,0:T(8,128)(2,1)S(1)}, bf16[1,128,2048]{2,1,0:T(8,128)(2,1)}) %tuple.17), branch_computations={%region_4.5_spmd, %region_5.8_spmd} | conditional | flops 550836352 | bytes 20278804 | solution.py:102
  33.2 0.1 broadcast_compare_fusion
  33.3 0.2 copy.33
  33.6 1.1 %copy.45 = bf16[16,8,16,128]{3,2,1,0:T(8,128)(2,1)S(1)} copy(bf16[16,8,16,128]{3,1,2,0:T(8,128)(2,1)} %bitcast.62) | data formatting | bytes 1048576 | tf_op jit(solution)/shard_map/cond
  34.7 0.9 %fusion = (f32[128,2,8]{0,2,1:T(8,128)S(1)}, f32[2,512,128,8]{2,1,3,0:T(8,128)S(1)}) fusion(pred[128,512]{0,1:T(8,128)(4,1)S(1)} %broadcast_compare_fusion, bf16[512,2,128,1]{0,2,3,1:T(8,128)(2,1)S(1)} %bitcast.61, bf16[128,2,8,128]{3,2,1,0:T(8,128)(2,1)S(1)} %bitcast.60), kind=kOutput, calls=%fused_computation.2 | convolution fusion | flops 271579136 | bytes 5054464 | tf_op jit(solution)/shard_map/cond/branch_1_fun/tgrd,sgd->tgrs/dot_general | solution.py:15
  35.6 1.0 %fusion.2 = f32[128,2,8]{0,2,1:T(8,128)S(1)} fusion(f32[2,512,128,8]{2,1,3,0:T(8,128)S(1)} %get-tuple-element.60, f32[128,2,8]{0,2,1:T(8,128)S(1)} %broadcast_maximum_fusion, pred[128,512]{0,1:T(8,128)(4,1)S(1)} %broadcast_compare_fusion), kind=kLoop, calls=%fused_computation.4 | loop fusion | flops 5240832 | bytes 4276224 | tf_op jit(solution)/shard_map/cond/branch_1_fun/reduce_sum | solution.py:23
  36.6 1.5 %fusion.9 = f32[128,2,8,128]{3,0,2,1:T(8,128)S(1)} fusion(bf16[512,2,128,1]{0,2,3,1:T(8,128)(2,1)S(1)} %bitcast.63, f32[2,512,128,8]{2,1,3,0:T(8,128)S(1)} %get-tuple-element.60, f32[128,2,8]{0,2,1:T(8,128)S(1)} %broadcast_maximum_fusion, pred[128,512]{0,1:T(8,128)(4,1)S(1)} %broadcast_compare_fusion, f32[128,2,8]{0,2,1:T(8,128)S(1)} %get-tuple-element.57), kind=kOutput, calls=%fused_computation.8 | convolution fusion | flops 273940480 | bytes 5586944 | tf_op jit(solution)/shard_map/cond/branch_1_fun/tgrs,sgd->tgrd/dot_general | solution.py:24
  38.1 0.3 copy.44
  38.5 0.1 divide_convert_fusion
  38.6 1.0 %copy.35 = bf16[1,128,2048]{2,1,0:T(8,128)(2,1)} copy(bf16[1,128,2048]{1,2,0:T(8,128)(2,1)S(1)} %bitcast.58) | data formatting | bytes 1048576
  39.6 0.2 fusion.25
  39.8 5.4 %psum.7 = f32[1,128]{1,0:T(1,128)} all-reduce(f32[1,128]{1,0:T(1,128)S(1)} %fusion.25), channel_id=1, replica_groups=mesh['dp'=4,'ctx'=4,'tp'=2] {'tp'}, use_global_device_ids=true, to_apply=%region_8.9 | all-reduce | flops 128 | bytes 1024 | tf_op jit(solution)/shard_map/psum | solution.py:112
  (9 shorter events, 0.1 us)
Async XLA Ops:
  4.2 11.8 %all-to-all-start = ((s32[4,4,1]{1,2,0:T(1,128)}), s32[4,4,1]{1,2,0:T(1,128)S(1)}, u32[]{:S(2)}, u32[]{:S(2)}) async-start(s32[4,4,1]{1,2,0:T(1,128)} %bitcast.9), calls=%async_computation | async-start | bytes 4096 | tf_op jit(solution)/shard_map/all_to_all | solution.py:64
  16.0 8.8 %all-to-all-start.1 = ((bf16[16,2,256]{2,1,0:T(2,128)(2,1)}), bf16[16,2,256]{2,1,0:T(2,128)(2,1)S(1)}, u32[]{:S(2)}, u32[]{:S(2)}) async-start(bf16[16,2,256]{2,1,0:T(2,128)(2,1)} %reshape.108), calls=%async_computation.1 | async-start | bytes 32768 | tf_op jit(solution)/shard_map/all_to_all | solution.py:63
